TPU v7x, 32 devices: a whole 2x2x4 slice. The times are simulated.
32 devices in a mesh: fsdp: 16 (over z, y, core), grp: 2 (over x).
Axes of the slice: x: 2, y: 2, z: 4, core: 2. Of those that a mesh axis runs over, the one named last changes fastest.
Arguments:
- hidden: bfloat16 [8192, 3072], P('fsdp', 'grp'), may hold values from -16 to 16
- queries: bfloat16 [8192, 1536], P('fsdp', 'grp'), may hold values from -6 to 6
- attn_keys: bfloat16 [8192, 1536], P('fsdp', 'grp'), may hold values from -6 to 6
- w_value: bfloat16 [1536, 3072], P('fsdp', 'grp'), may hold values from -1 to 1
- w_out: bfloat16 [1536, 3072], P('fsdp', 'grp'), may hold values from -1 to 1
- alpha: float32 [3072], P('grp'), may hold values from 0.05 to 0.5
- out_grad: bfloat16 [8192, 3072], P('fsdp', 'grp'), may hold values from -6 to 6
Outputs:
- new_hidden: bfloat16 [8192, 3072], P('fsdp', 'grp')
- grad_hidden: bfloat16 [8192, 3072], P('fsdp', 'grp')
- grad_queries: bfloat16 [8192, 1536], P('fsdp', 'grp')
- grad_keys: bfloat16 [8192, 1536], P('fsdp', 'grp')
- grad_w_value: float32 [1536, 3072], P('fsdp', 'grp')
- grad_w_out: float32 [1536, 3072], P('fsdp', 'grp')
All inputs are finite; a program needn't handle non-finite values.
Results may differ from a plain program's by a relative error of at most 0.012.
The roundings to bfloat16 on the way count: a program that leaves them out, or rounds other values in their place, can miss the bound.
Values may be sent and summed in bfloat16 or wider, within the bound.
A program may use at most 192 MiB of HBM per device.

v0:
```python
import jax
import jax.numpy as jnp
from jax import lax
from jax.experimental import pallas as pl
from jax.experimental.pallas import tpu as pltpu
from jax.sharding import PartitionSpec as P

D = 3072
HS = 128


EPS = 1e-06


def contract_last(left, right):
    return lax.dot_general(
        left, right, (((1,), (1,)), ((), ())), preferred_element_type=jnp.float32
    )


def contract_first(left, right):
    return lax.dot_general(
        left, right, (((0,), (0,)), ((), ())), preferred_element_type=jnp.float32
    )


def cost(flops, nbytes):
    return pl.CostEstimate(flops=flops, bytes_accessed=nbytes, transcendentals=0)


def probs_kernel(q_ref, k_ref, probs_ref):
    length = q_ref.shape[0]
    score_scale = q_ref.shape[1] ** (-0.5)
    scores = contract_last(q_ref[...], k_ref[...]) * score_scale
    row_pos = lax.broadcasted_iota(jnp.int32, (length, length), 0)
    col_pos = lax.broadcasted_iota(jnp.int32, (length, length), 1)
    scores = jnp.where(row_pos >= col_pos, scores, -1e30)
    row_peak = jnp.max(scores, axis=1, keepdims=True)
    exp_terms = jnp.exp(scores - row_peak)
    probs_ref[0] = exp_terms * (1.0 / jnp.sum(exp_terms, axis=1, keepdims=True))


def forward_kernel(probs_ref, part_ref, recv_ref, scale_ref, attn_ref, values_ref):
    values = (part_ref[...] + recv_ref[...].astype(jnp.float32)) * scale_ref[...]
    values_b = values.astype(jnp.bfloat16)
    values_ref[...] = values_b
    attn_ref[...] = jnp.dot(
        probs_ref[0].astype(jnp.bfloat16), values_b, preferred_element_type=jnp.float32
    ).astype(jnp.bfloat16)


def backward_kernel(
    probs_ref, q_ref, k_ref, v_ref, part_ref, recv_ref, gq_ref, gk_ref, gv_ref
):
    score_scale = q_ref.shape[1] ** (-0.5)
    grad_head = (part_ref[...] + recv_ref[...].astype(jnp.float32)).astype(jnp.bfloat16)
    probs = probs_ref[0]
    grad_prob = contract_last(grad_head, v_ref[...])
    row_delta = jnp.sum(probs * grad_prob, axis=1, keepdims=True)
    grad_score = (probs * (grad_prob - row_delta)).astype(jnp.bfloat16)
    gv_ref[...] = contract_first(probs.astype(jnp.bfloat16), grad_head).astype(jnp.bfloat16)
    gq_ref[...] = (
        jnp.dot(grad_score, k_ref[...], preferred_element_type=jnp.float32) * score_scale
    ).astype(jnp.bfloat16)
    gk_ref[...] = (contract_first(grad_score, q_ref[...]) * score_scale).astype(jnp.bfloat16)


def head_spec(length):
    return pl.BlockSpec((length, HS), lambda h: (0, h))


def square_spec(length):
    return pl.BlockSpec((1, length, length), lambda h: (h, 0, 0))


def head_probs(queries, keys):
    length, width = queries.shape
    heads = width // HS
    return pl.pallas_call(
        probs_kernel,
        grid=(heads,),
        in_specs=[head_spec(length)] * 2,
        out_specs=square_spec(length),
        out_shape=jax.ShapeDtypeStruct((heads, length, length), jnp.float32),
        cost_estimate=cost(heads * 30 * HS * length * length, 4 * heads * length * length),
    )(queries, keys)


def attend(probs, part, recv, scale):
    length, width = part.shape
    heads = width // HS
    one = head_spec(length)
    shape = jax.ShapeDtypeStruct((length, width), jnp.bfloat16)
    return pl.pallas_call(
        forward_kernel,
        grid=(heads,),
        in_specs=[square_spec(length), one, one, pl.BlockSpec((1, HS), lambda h: (0, h))],
        out_specs=[one, one],
        out_shape=[shape, shape],
        cost_estimate=cost(heads * 4 * HS * length * length, 6 * heads * length * length),
    )(probs, part, recv, scale)


def attend_backward(probs, queries, keys, values, part, recv):
    length, width = part.shape
    heads = width // HS
    one = head_spec(length)
    shape = jax.ShapeDtypeStruct((length, width), jnp.bfloat16)
    return pl.pallas_call(
        backward_kernel,
        grid=(heads,),
        in_specs=[square_spec(length)] + [one] * 5,
        out_specs=[one] * 3,
        out_shape=[shape] * 3,
        cost_estimate=cost(heads * 30 * HS * length * length, 6 * heads * length * length),
    )(probs, queries, keys, values, part, recv)


def shards(hidden, queries, attn_keys, w_value, w_out, alpha, out_grad):
    groups = lax.axis_size("grp")
    assert groups == 2
    me = lax.axis_index("grp")
    swap = [(0, 1), (1, 0)]

    def exchange(block):
        return lax.ppermute(block, "grp", swap)

    def mine_and_other(weight):
        rows = weight.shape[0] // groups
        return (
            lax.dynamic_slice_in_dim(weight, me * rows, rows, 0),
            lax.dynamic_slice_in_dim(weight, (1 - me) * rows, rows, 0),
        )

    def in_order(mine, other):
        return jnp.concatenate(
            (jnp.where(me == 0, mine, other), jnp.where(me == 0, other, mine)), axis=1
        )

    raw_v = lax.all_gather(w_value, "fsdp", axis=0, tiled=True)
    value_rows = w_value.astype(jnp.float32)
    out_rows = w_out.astype(jnp.float32)
    own_sums = jnp.stack(
        (jnp.sum(value_rows * value_rows, axis=1), jnp.sum(out_rows * out_rows, axis=1))
    )
    own_sums = own_sums + exchange(own_sums)
    norms = jnp.sqrt(own_sums + EPS)
    norm_v = norms[0][:, None]
    norm_o = norms[1][:, None]
    unit_v = value_rows / norm_v
    unit_o = out_rows / norm_o
    weight_o = lax.all_gather(unit_o.astype(jnp.bfloat16), "fsdp", axis=0, tiled=True)
    probs = head_probs(queries, attn_keys)

    raw_mine, raw_other = mine_and_other(raw_v)
    value_recv = exchange(contract_last(hidden, raw_other).astype(jnp.bfloat16))
    value_part = contract_last(hidden, raw_mine)
    raw_rows = raw_v.astype(jnp.float32)
    raw_sums = jnp.sum(raw_rows * raw_rows, axis=1)
    all_norm_v = jnp.sqrt(raw_sums + exchange(raw_sums) + EPS)
    width = queries.shape[1]
    scale = 1.0 / lax.dynamic_slice_in_dim(all_norm_v, me * width, width, 0)
    attn_mine, values = attend(probs, value_part, value_recv, scale[None, :])
    weight_v = (raw_v.astype(jnp.float32) / all_norm_v[:, None]).astype(jnp.bfloat16)
    attn_all = in_order(attn_mine, exchange(attn_mine))
    proj = jnp.dot(attn_all, weight_o, preferred_element_type=jnp.float32)
    hidden_f = hidden.astype(jnp.float32)
    keep_rate = 1.0 - alpha
    grad_out = out_grad.astype(jnp.float32)
    moments = jnp.stack(
        (
            jnp.sum(proj * proj, axis=1),
            jnp.sum(keep_rate * keep_rate * hidden_f * hidden_f, axis=1),
            jnp.sum(keep_rate * alpha * hidden_f * proj, axis=1),
            jnp.sum(alpha * alpha * proj * proj, axis=1),
            jnp.sum(grad_out * keep_rate * hidden_f, axis=1),
            jnp.sum(grad_out * alpha * proj, axis=1),
        )
    )
    moments = moments + exchange(moments)
    proj_rs = lax.rsqrt(moments[0] / D + EPS)[:, None]
    cross_sum = moments[2][:, None]
    alpha_sum = moments[3][:, None]
    mix_mean = (moments[1][:, None] + 2.0 * proj_rs * cross_sum + proj_rs * proj_rs * alpha_sum) / D
    mix_rs = lax.rsqrt(mix_mean + EPS)
    mixed = hidden_f + alpha * (proj * proj_rs - hidden_f)
    new_hidden = (mixed * mix_rs).astype(jnp.bfloat16)
    grad_mean = (moments[4][:, None] + proj_rs * moments[5][:, None]) / D
    grad_mix = mix_rs * (grad_out - mixed * mix_rs * mix_rs * grad_mean)
    grad_pn = grad_mix * alpha
    proj_mean = (
        mix_rs * moments[5][:, None]
        - mix_rs * mix_rs * mix_rs * grad_mean * (cross_sum + proj_rs * alpha_sum)
    ) / D
    grad_res = grad_mix * keep_rate
    grad_proj = proj_rs * (grad_pn - proj * proj_rs * proj_rs * proj_mean)
    grad_proj_b = grad_proj.astype(jnp.bfloat16)
    out_mine, out_other = mine_and_other(weight_o)
    grad_recv = exchange(contract_last(grad_proj_b, out_other).astype(jnp.bfloat16))
    grad_part = contract_last(grad_proj_b, out_mine)
    gw_o_own = lax.psum_scatter(
        contract_first(attn_all, grad_proj_b).astype(jnp.bfloat16),
        "fsdp",
        scatter_dimension=0,
        tiled=True,
    ).astype(jnp.float32)
    grad_q, grad_k, grad_v = attend_backward(
        probs, queries, attn_keys, values, grad_part, grad_recv
    )
    grad_values = in_order(grad_v, exchange(grad_v))
    gw_v_own = lax.psum_scatter(
        contract_first(grad_values, hidden).astype(jnp.bfloat16),
        "fsdp",
        scatter_dimension=0,
        tiled=True,
    ).astype(jnp.float32)
    grad_hidden = (
        grad_res + jnp.dot(grad_values, weight_v, preferred_element_type=jnp.float32)
    ).astype(jnp.bfloat16)
    dot_o = jnp.sum(gw_o_own * unit_o, axis=1, keepdims=True)
    dot_o = dot_o + exchange(dot_o)
    grad_w_out = (gw_o_own - unit_o * dot_o) / norm_o
    dot_v = jnp.sum(gw_v_own * unit_v, axis=1, keepdims=True)
    dot_v = dot_v + exchange(dot_v)
    grad_w_value = (gw_v_own - unit_v * dot_v) / norm_v
    return (new_hidden, grad_hidden, grad_q, grad_k, grad_w_value, grad_w_out)


def solution(mesh):
    placed = (
        P("fsdp", "grp"),
        P("fsdp", "grp"),
        P("fsdp", "grp"),
        P("fsdp", "grp"),
        P("fsdp", "grp"),
        P("grp"),
        P("fsdp", "grp"),
    )
    return jax.shard_map(
        shards,
        mesh=mesh,
        in_specs=placed,
        out_specs=(
            P("fsdp", "grp"),
            P("fsdp", "grp"),
            P("fsdp", "grp"),
            P("fsdp", "grp"),
            P("fsdp", "grp"),
            P("fsdp", "grp"),
        ),
        check_vma=False,
    )
```

profile of v0, /device:TPU:8, one launch (start us, length us, event | category | flops | bytes accessed | tf_op | source)
XLA Modules:
  0.0 306.1 jit_solution(12410311238871354410)
XLA Ops:
  10.2 1.6 collective-permute-start.3
  11.8 2.1 collective-permute-done.3
  13.9 1.8 fusion.63
  15.8 7.0 %shard_map.118.probs_ref = f32[6,512,512]{2,1,0:T(8,128)} custom-call(bf16[512,768]{1,0:T(8,128)(2,1)} %q_ref.3, bf16[512,768]{1,0:T(8,128)(2,1)} %k_ref.3), custom_call_target="tpu_custom_call" | custom-call | flops 6039797760 | bytes 6291456 | tf_op jit(solution)/shard_map/pallas_call | solution.py:79
  22.8 41.8 %all-gather.3.cloned.1.call-done = bf16[1536,1536]{1,0:T(8,128)(2,1)} async-done(((bf16[96,1536]{1,0:T(8,128)(2,1)}), bf16[1536,1536]{1,0:T(8,128)(2,1)}) %all-gather.3.cloned.1.call-update) | async-done | bytes 4718608 | tf_op jit(solution)/shard_map/all_gather | solution.py:140
  64.6 3.2 %fusion.37 = bf16[512,768]{1,0:T(8,128)(2,1)S(1)} fusion(bf16[512,1536]{1,0:T(8,128)(2,1)S(1)} %copy-done.5, bf16[1536,1536]{1,0:T(8,128)(2,1)} %all-gather.3.cloned.1.call-done, s32[]{:T(128)S(6)} %select_n.31), kind=kOutput, calls=%fused_computation.44 | convolution fusion | flops 1208352768 | bytes 4718596 | tf_op jit(solution)/shard_map/dot_general | solution.py:16
  67.8 1.5 collective-permute-start
  71.0 2.6 fusion.28.part_ref
  73.5 14.2 %collective-permute-done.1 = f32[1536]{0:T(1024)S(1)} collective-permute-done((f32[1536]{0:T(1024)S(1)}, f32[1536]{0:T(1024)S(1)}, u32[]{:S(2)}, u32[]{:S(2)}) %collective-permute-start.1) | collective-permute-done | bytes 6176 | tf_op jit(solution)/shard_map/ppermute | solution.py:126
  89.3 6.9 %shard_map.119 = (bf16[512,768]{1,0:T(8,128)(2,1)}, bf16[512,768]{1,0:T(8,128)(2,1)}) custom-call(f32[6,512,512]{2,1,0:T(8,128)} %shard_map.118.probs_ref, f32[512,768]{1,0:T(8,128)} %fusion.28.part_ref, bf16[512,768]{1,0:T(8,128)(2,1)} %copy-done.10, f32[1,768]{1,0:T(1,128)} %broadcast_in_dim.6.scale_ref), custom_call_target="tpu_custom_call" | custom-call | flops 805306368 | bytes 9437184 | tf_op jit(solution)/shard_map/pallas_call | solution.py:94
  97.7 17.5 %collective-permute-done.2 = bf16[512,768]{1,0:T(8,128)(2,1)S(1)} collective-permute-done((bf16[512,768]{1,0:T(8,128)(2,1)}, bf16[512,768]{1,0:T(8,128)(2,1)S(1)}, u32[]{:S(2)}, u32[]{:S(2)}) %collective-permute-start.2) | collective-permute-done | bytes 786464 | tf_op jit(solution)/shard_map/ppermute | solution.py:126
  115.2 2.4 broadcast_select_fusion.3
  117.6 1.5 all-gather.5.cloned.1.call-done
  119.1 7.5 %fusion.9 = (f32[512]{0:T(512)S(1)}, f32[512]{0:T(512)S(1)}, f32[512]{0:T(512)S(1)}, f32[512]{0:T(512)S(1)}, f32[512]{0:T(512)S(1)}, /*index=5*/f32[512]{0:T(512)S(1)}, f32[512,1536]{1,0:T(8,128)S(1)}) fusion(bf16[512,1536]{1,0:T(8,128)(2,1)} %param.13, f32[1536]{0:T(1024)S(1)} %copy-done.14, f32[1536]{0:T(1024)S(1)} %get-tuple-element.35, ...), kind=kOutput, calls=%fused_computation.20 | convolution fusion | flops 2434003968 | bytes 12625920 | tf_op jit(solution)/shard_map/dot_general | solution.py:166
  126.7 1.5 collective-permute-start.4
  128.2 2.3 collective-permute-done.4
  130.6 4.5 %multiply_convert_fusion = (bf16[512,1536]{1,0:T(8,128)(2,1)S(1)}, bf16[512,1536]{1,0:T(8,128)(2,1)}) fusion(f32[512,1536]{1,0:T(8,128)S(1)} %get-tuple-element.43, bf16[512,1536]{1,0:T(8,128)(2,1)} %param.13, f32[512]{0:T(512)S(1)} %get-tuple-element.36, f32[512]{0:T(512)S(1)} %get-tuple-element.40, f32[512]{0:T(512)S(1)} %get-tuple-element.37, ...), kind=kLoop, calls=%fused_computation.28 | loop fusion | flops 14155776 | bytes 9451520 | tf_op jit(solution)/shard_map/convert_element_type | solution.py:197
  136.2 4.3 %convolution_convert_fusion = bf16[1536,1536]{1,0:T(8,128)(2,1)} fusion(bf16[512,1536]{1,0:T(8,128)(2,1)S(1)} %get-tuple-element.22, bf16[512,768]{1,0:T(8,128)(2,1)S(1)} %copy-done.12, bf16[512,768]{1,0:T(8,128)(2,1)S(1)} %copy-done.11), kind=kOutput, calls=%fused_computation.4 | convolution fusion | flops 2421424128 | bytes 7864320 | tf_op jit(solution)/shard_map/dot_general | solution.py:22
  141.9 3.1 %fusion.34 = bf16[512,768]{1,0:T(8,128)(2,1)S(1)} fusion(bf16[512,1536]{1,0:T(8,128)(2,1)S(1)} %copy-done.8, bf16[1536,1536]{1,0:T(8,128)(2,1)} %all-gather.5.cloned.1.call-done, s32[]{:T(128)S(6)} %select_n.31), kind=kOutput, calls=%fused_computation.43 | convolution fusion | flops 1208352768 | bytes 4718596 | tf_op jit(solution)/shard_map/dot_general | solution.py:16
  145.0 1.5 collective-permute-start.5
  146.5 4.4 %fusion.22.part_ref = f32[512,768]{1,0:T(8,128)} fusion(bf16[512,1536]{1,0:T(8,128)(2,1)S(1)} %copy-done.8, bf16[1536,1536]{1,0:T(8,128)(2,1)} %all-gather.5.cloned.1.call-done, s32[]{:T(128)S(6)} %select_n.30), kind=kOutput, calls=%fused_computation.33 | convolution fusion | flops 1207959552 | bytes 5505028 | tf_op jit(solution)/shard_map/dot_general | solution.py:16
  150.9 12.7 %collective-permute-done.5.recv_ref = bf16[512,768]{1,0:T(8,128)(2,1)S(1)} collective-permute-done((bf16[512,768]{1,0:T(8,128)(2,1)S(1)}, bf16[512,768]{1,0:T(8,128)(2,1)S(1)}, u32[]{:S(2)}, u32[]{:S(2)}) %collective-permute-start.5) | collective-permute-done | bytes 786464 | tf_op jit(solution)/shard_map/ppermute | solution.py:126
  164.5 9.6 %shard_map.120 = (bf16[512,768]{1,0:T(8,128)(2,1)}, bf16[512,768]{1,0:T(8,128)(2,1)}, bf16[512,768]{1,0:T(8,128)(2,1)}) custom-call(f32[6,512,512]{2,1,0:T(8,128)} %shard_map.118.probs_ref, bf16[512,768]{1,0:T(8,128)(2,1)} %q_ref.3, bf16[512,768]{1,0:T(8,128)(2,1)} %k_ref.3, bf16[512,768]{1,0:T(8,128)(2,1)} %get-tuple-element.12.v_ref, ...), custom_call_target="tpu_custom_call" | custom-call | flops 6039797760 | bytes 9437184 | tf_op jit(solution)/shard_map/pallas_call | solution.py:109
  174.1 1.5 collective-permute-start.6
  175.6 16.5 %collective-permute-done.6 = bf16[512,768]{1,0:T(8,128)(2,1)S(1)} collective-permute-done((bf16[512,768]{1,0:T(8,128)(2,1)}, bf16[512,768]{1,0:T(8,128)(2,1)S(1)}, u32[]{:S(2)}, u32[]{:S(2)}) %collective-permute-start.6) | collective-permute-done | bytes 786464 | tf_op jit(solution)/shard_map/ppermute | solution.py:126
  194.2 4.3 %convolution_convert_fusion.1 = bf16[1536,1536]{1,0:T(8,128)(2,1)} fusion(bf16[512,1536]{1,0:T(8,128)(2,1)S(1)} %copy-done.6, bf16[512,768]{1,0:T(8,128)(2,1)S(1)} %get-tuple-element.25, bf16[512,768]{1,0:T(8,128)(2,1)S(1)} %get-tuple-element.24), kind=kOutput, calls=%fused_computation.5 | convolution fusion | flops 2421424128 | bytes 7864320 | tf_op jit(solution)/shard_map/dot_general | solution.py:22
  198.6 15.6 %reduce-scatter.5.cloned.1.call-done = bf16[96,1536]{1,0:T(8,128)(2,1)} async-done(((bf16[1536,1536]{1,0:T(8,128)(2,1)}), bf16[96,1536]{1,0:T(8,128)(2,1)}) %reduce-scatter.5.cloned.1.call-update) | async-done | bytes 294928 | tf_op jit(solution)/shard_map/reduce_scatter | solution.py:201
  215.5 1.5 collective-permute-start.8
  217.0 8.2 %fusion.17 = bf16[512,1536]{1,0:T(8,128)(2,1)} fusion(bf16[1536,1536]{1,0:T(8,128)(2,1)} %all-gather.3.cloned.1.call-done, f32[1536]{0:T(1024)S(1)} %add_sqrt_fusion, bf16[512,1536]{1,0:T(8,128)(2,1)S(1)} %copy-done.4, f32[512]{0:T(512)S(1)} %get-tuple-element.40, f32[512]{0:T(512)S(1)} %get-tuple-element.37, f32[1536]{0:T(1024)S(1)} %get-tuple-element.38, ...), kind=kOutput, calls=%fused_computation.30 | convolution fusion | flops 2437152768 | bytes 14180352 | tf_op jit(solution)/shard_map/dot_general | solution.py:218
  225.2 67.5 %reduce-scatter.3.cloned.1.call-done = bf16[96,1536]{1,0:T(8,128)(2,1)} async-done(((bf16[1536,1536]{1,0:T(8,128)(2,1)}), bf16[96,1536]{1,0:T(8,128)(2,1)}) %reduce-scatter.3.cloned.1.call-update) | async-done | bytes 294928 | tf_op jit(solution)/shard_map/reduce_scatter | solution.py:211
  293.9 1.6 collective-permute-start.7
  297.6 2.0 fusion.44
  (65 shorter events, 18.0 us)
Async XLA Ops:
  7.2 57.4 %all-gather.3.cloned.1.call-start = ((), (), s32[]{:S(2)}) async-start(), calls=%async_computation.2 | async-start | bytes 5013504 | tf_op jit(solution)/shard_map/all_gather | solution.py:140
  7.9 111.2 %all-gather.5.cloned.1.call-start = ((), (), s32[]{:S(2)}) async-start(), calls=%async_computation.3 | async-start | bytes 5013504 | tf_op jit(solution)/shard_map/all_gather | solution.py:152
  10.2 3.6 %collective-permute-start.3 = (f32[2,96]{1,0:T(2,128)S(1)}, f32[2,96]{1,0:T(2,128)S(1)}, u32[]{:S(2)}, u32[]{:S(2)}) collective-permute-start(f32[2,96]{1,0:T(2,128)S(1)} %pad_maximum_fusion.6), channel_id=1, source_target_pairs={{0,1},{1,0},{2,3},{3,2},{4,5},{5,4},{6,7},{7,6},{8,9},{9,8},{10,11... | collective-permute-start | bytes 2312 | tf_op jit(solution)/shard_map/ppermute | solution.py:126
  15.7 198.5 %reduce-scatter.5.cloned.1.call-start = ((), (), s32[]{:S(2)}) async-start(), calls=%async_computation.5 | async-start | bytes 5013504 | tf_op jit(solution)/shard_map/reduce_scatter | solution.py:201
  15.8 48.8 %copy-start.5 = (bf16[512,1536]{1,0:T(8,128)(2,1)S(1)}, bf16[512,1536]{1,0:T(8,128)(2,1)}, u32[]{:S(2)}) copy-start(bf16[512,1536]{1,0:T(8,128)(2,1)} %param.7) | copy-start | bytes 4718596
  64.6 4.8 %copy-start = (bf16[1536,1536]{1,0:T(8,128)(2,1)S(1)}, bf16[1536,1536]{1,0:T(8,128)(2,1)}, u32[]{:S(2)}) copy-start(bf16[1536,1536]{1,0:T(8,128)(2,1)} %all-gather.3.cloned.1.call-done) | copy-start | bytes 14155780
  67.8 20.6 %collective-permute-start = (bf16[512,768]{1,0:T(8,128)(2,1)S(1)}, bf16[512,768]{1,0:T(8,128)(2,1)S(1)}, u32[]{:S(2)}, u32[]{:S(2)}) collective-permute-start(bf16[512,768]{1,0:T(8,128)(2,1)S(1)} %fusion.37), channel_id=1, source_target_pairs={{0,1},{1,0},{2,3},{3,2},{4,5},{5,4},{6,7},{7,6},{8,9},{9,8},{10,11... | collective-permute-start | bytes 2359304 | tf_op jit(solution)/shard_map/ppermute | solution.py:126
  70.4 17.4 %collective-permute-start.1 = (f32[1536]{0:T(1024)S(1)}, f32[1536]{0:T(1024)S(1)}, u32[]{:S(2)}, u32[]{:S(2)}) collective-permute-start(f32[1536]{0:T(1024)S(1)} %fusion), channel_id=1, source_target_pairs={{0,1},{1,0},{2,3},{3,2},{4,5},{5,4},{6,7},{7,6},{8,9},{9,8},{10,11... | collective-permute-start | bytes 18440 | tf_op jit(solution)/shard_map/ppermute | solution.py:126
  88.5 9.3 %copy-start.14 = (f32[1536]{0:T(1024)S(1)}, f32[1536]{0:T(1024)}, u32[]{:S(2)}) copy-start(f32[1536]{0:T(1024)} %param.12) | copy-start | bytes 18436
  88.5 0.9 copy-start.10
  96.2 19.0 %collective-permute-start.2 = (bf16[512,768]{1,0:T(8,128)(2,1)}, bf16[512,768]{1,0:T(8,128)(2,1)S(1)}, u32[]{:S(2)}, u32[]{:S(2)}) collective-permute-start(bf16[512,768]{1,0:T(8,128)(2,1)} %get-tuple-element.11), channel_id=1, source_target_pairs={{0,1},{1,0},{2,3},{3,2},{4,5},{5,4},{6,7},{7,6},{8,9},{9,8},{10,11... | collective-permute-start | bytes 2359304 | tf_op jit(solution)/shard_map/ppermute | solution.py:126
  126.6 8.4 %copy-start.3 = (f32[512,1536]{1,0:T(8,128)}, f32[512,1536]{1,0:T(8,128)S(1)}, u32[]{:S(2)}) copy-start(f32[512,1536]{1,0:T(8,128)S(1)} %get-tuple-element.43) | copy-start | bytes 9437188
  126.7 3.8 %collective-permute-start.4 = (f32[6,512]{1,0:T(8,128)S(1)}, f32[6,512]{1,0:T(8,128)S(1)}, u32[]{:S(2)}, u32[]{:S(2)}) collective-permute-start(f32[6,512]{1,0:T(8,128)S(1)} %stack.39), channel_id=1, source_target_pairs={{0,1},{1,0},{2,3},{3,2},{4,5},{5,4},{6,7},{7,6},{8,9},{9,8},{10,11... | collective-permute-start | bytes 36872 | tf_op jit(solution)/shard_map/ppermute | solution.py:126
  130.5 5.6 %copy-start.11 = (bf16[512,768]{1,0:T(8,128)(2,1)S(1)}, bf16[512,768]{1,0:T(8,128)(2,1)}, u32[]{:S(2)}) copy-start(bf16[512,768]{1,0:T(8,128)(2,1)} %get-tuple-element.26) | copy-start | bytes 2359300
  130.6 5.6 %copy-start.12 = (bf16[512,768]{1,0:T(8,128)(2,1)S(1)}, bf16[512,768]{1,0:T(8,128)(2,1)}, u32[]{:S(2)}) copy-start(bf16[512,768]{1,0:T(8,128)(2,1)} %get-tuple-element.27) | copy-start | bytes 2359300
  135.0 1.1 copy-start.7
  140.5 1.4 copy-start.8
  140.5 152.2 %reduce-scatter.3.cloned.1.call-start = ((), (), s32[]{:S(2)}) async-start(), calls=%async_computation.4 | async-start | bytes 5013504 | tf_op jit(solution)/shard_map/reduce_scatter | solution.py:211
  145.0 18.6 %collective-permute-start.5 = (bf16[512,768]{1,0:T(8,128)(2,1)S(1)}, bf16[512,768]{1,0:T(8,128)(2,1)S(1)}, u32[]{:S(2)}, u32[]{:S(2)}) collective-permute-start(bf16[512,768]{1,0:T(8,128)(2,1)S(1)} %fusion.34), channel_id=1, source_target_pairs={{0,1},{1,0},{2,3},{3,2},{4,5},{5,4},{6,7},{7,6},{8,9},{9,8},{10,11... | collective-permute-start | bytes 2359304 | tf_op jit(solution)/shard_map/ppermute | solution.py:126
  163.6 0.9 copy-start.15
  174.0 20.2 %copy-start.6 = (bf16[512,1536]{1,0:T(8,128)(2,1)S(1)}, bf16[512,1536]{1,0:T(8,128)(2,1)}, u32[]{:S(2)}) copy-start(bf16[512,1536]{1,0:T(8,128)(2,1)} %param.7) | copy-start | bytes 4718596
  174.1 18.0 %collective-permute-start.6 = (bf16[512,768]{1,0:T(8,128)(2,1)}, bf16[512,768]{1,0:T(8,128)(2,1)S(1)}, u32[]{:S(2)}, u32[]{:S(2)}) collective-permute-start(bf16[512,768]{1,0:T(8,128)(2,1)} %get-tuple-element.13), channel_id=1, source_target_pairs={{0,1},{1,0},{2,3},{3,2},{4,5},{5,4},{6,7},{7,6},{8,9},{9,8},{10,11... | collective-permute-start | bytes 2359304 | tf_op jit(solution)/shard_map/ppermute | solution.py:126
  193.3 0.9 copy-start.13
  198.6 15.7 %copy-start.1 = (bf16[96,1536]{1,0:T(8,128)(2,1)S(1)}, bf16[96,1536]{1,0:T(8,128)(2,1)}, u32[]{:S(2)}) copy-start(bf16[96,1536]{1,0:T(8,128)(2,1)} %param.11) | copy-start | bytes 884740
  198.6 18.4 %copy-start.4 = (bf16[512,1536]{1,0:T(8,128)(2,1)S(1)}, bf16[512,1536]{1,0:T(8,128)(2,1)}, u32[]{:S(2)}) copy-start(bf16[512,1536]{1,0:T(8,128)(2,1)} %param.13) | copy-start | bytes 4718596
  215.5 77.2 %copy-start.2 = (bf16[96,1536]{1,0:T(8,128)(2,1)S(1)}, bf16[96,1536]{1,0:T(8,128)(2,1)}, u32[]{:S(2)}) copy-start(bf16[96,1536]{1,0:T(8,128)(2,1)} %param.10) | copy-start | bytes 884740
  215.5 80.0 %copy-start.9 = (bf16[96,1536]{1,0:T(8,128)(2,1)S(1)}, bf16[96,1536]{1,0:T(8,128)(2,1)}, u32[]{:S(2)}) copy-start(bf16[96,1536]{1,0:T(8,128)(2,1)} %reduce-scatter.5.cloned.1.call-done) | copy-start | bytes 884740
  215.5 9.7 %collective-permute-start.8 = (f32[96,1]{0,1:T(1,128)S(1)}, f32[96,1]{0,1:T(1,128)S(1)}, u32[]{:S(2)}, u32[]{:S(2)}) collective-permute-start(f32[96,1]{0,1:T(1,128)S(1)} %bitcast.55), channel_id=1, source_target_pairs={{0,1},{1,0},{2,3},{3,2},{4,5},{5,4},{6,7},{7,6},{8,9},{9,8},{10,11... | collective-permute-start | bytes 1160 | tf_op jit(solution)/shard_map/ppermute | solution.py:126
  293.9 3.6 %collective-permute-start.7 = (f32[96,1]{0,1:T(1,128)S(1)}, f32[96,1]{0,1:T(1,128)S(1)}, u32[]{:S(2)}, u32[]{:S(2)}) collective-permute-start(f32[96,1]{0,1:T(1,128)S(1)} %bitcast.56), channel_id=1, source_target_pairs={{0,1},{1,0},{2,3},{3,2},{4,5},{5,4},{6,7},{7,6},{8,9},{9,8},{10,11... | collective-permute-start | bytes 1160 | tf_op jit(solution)/shard_map/ppermute | solution.py:126
Sparse Core Ops, SparseCore 0:
  10.3 54.2 all-gather.2
  67.4 51.6 all-gather.4
  140.6 73.5 reduce-scatter.4
  217.9 74.7 reduce-scatter.2
where the time goes:
time: 309 us; the launch traced here: 306 us
  waiting for transfers between devices  194 us (63%)
  matrix products  37.6 us (12%)
  Pallas kernels  23.5 us (8%)
  other arithmetic  18.7 us (6%)
  between operations  13.9 us (4%)
  starting transfers between devices  13.1 us (4%)
  local copies, waits for them, and re-layouts  5.67 us (2%)
    reduce_scatter x1, waiting for transfers between devices, shards(): lax.psum_scatter(contract_first(grad_values, hidden).astype(jnp.bfloat16)...  67.5 us
    ppermute x9, waiting for transfers between devices, exchange(): return lax.ppermute(block, 'grp', swap)  66.4 us
    all_gather x1, waiting for transfers between devices, shards(): raw_v = lax.all_gather(w_value, 'fsdp', axis=0, tiled=True)  41.8 us
    reduce_scatter x1, waiting for transfers between devices, shards(): lax.psum_scatter(contract_first(attn_all, grad_proj_b).astype(jnp.bfloat1...  15.6 us
    dot_general x4, matrix products, contract_last(): lax.dot_general(left, right, (((1,), (1,)), ((), ())), preferred_element_...  13.2 us
    ppermute x9, starting transfers between devices, exchange(): return lax.ppermute(block, 'grp', swap)  12.8 us
    pallas_call x1, Pallas kernels, attend_backward(): pl.pallas_call(backward_kernel, grid=(heads,), in_specs=[square_spec(leng...  9.56 us
    dot_general x2, matrix products, contract_first(): lax.dot_general(left, right, (((0,), (0,)), ((), ())), preferred_element_...  8.63 us
  transfers between devices with their start and end apart: 13, of which 11 were waited for; matrix products, arithmetic and copies ran while one was open for 12% of the time, Pallas kernels for 8%

commit v1 on v0

--- a/solution.py
+++ b/solution.py
@@ -226,6 +226,580 @@
     return (new_hidden, grad_hidden, grad_q, grad_k, grad_w_value, grad_w_out)
 
 
+MESH = pl.DeviceIdType.MESH
+BLOCK = 256
+BF = jnp.bfloat16
+F32 = jnp.float32
+
+
+def nearest(z, s, count):
+    reach = jnp.minimum(z, count - 1 - z)
+    both = z - (s + 1) // 2 if s % 2 else z + s // 2
+    rest = jnp.where(z <= count - 1 - z, s, count - 1 - s)
+    return jnp.where(s <= 2 * reach, both, rest)
+
+
+def layer_kernel(
+    hid, q, k, wv, wo, alpha, og,
+    nh, gh, gq, gk, gwv, gwo,
+    all_v, all_o, probs, nrm, part, xsend, xrecv, vals, attn, proj, gpb, mom, momx, gval,
+    grad_s, big_o, ra, rb, rc, acc, fin, dots,
+    z_in, z_out, y_in, y_out, c_in, c_out,
+    a_in, a_out, b_in, b_out, r_in, r_out, x_in, x_out, s_in, s_out,
+):
+    tokens, width = hid.shape
+    rows = wv.shape[0]
+    heads = part.shape[0]
+    devices = all_v.shape[0] // rows
+    line = devices // 4
+    unit = 4 * rows
+    per_unit = unit // HS
+    own_units = line // 2
+    score_scale = HS ** (-0.5)
+    full = 2 * width
+
+    me = lax.axis_index("fsdp")
+    g = lax.axis_index("grp")
+    z = me // 4
+    y = lax.rem(me // 2, 2)
+    c = lax.rem(me, 2)
+    right, left = me + 4, me - 4
+    across = z * 4 + (1 - y) * 2 + c
+    sibling = z * 4 + y * 2 + (1 - c)
+    low = g * own_units
+    other_low = (1 - g) * own_units
+
+    def copy(src, dst, out_sem, in_sem, dev):
+        return pltpu.make_async_remote_copy(
+            src_ref=src, dst_ref=dst, send_sem=out_sem, recv_sem=in_sem,
+            device_id=dev, device_id_type=MESH,
+        )
+
+    def xcopy(src, dst, kind, h):
+        return copy(src, dst, x_out.at[kind, h], x_in.at[kind, h], {"grp": 1 - g})
+
+    def scopy(src, dst, i):
+        return copy(src, dst, s_out.at[i], s_in.at[i], {"grp": 1 - g})
+
+    barrier = pltpu.get_barrier_semaphore()
+
+    def greet(dev):
+        pl.semaphore_signal(barrier, inc=1, device_id=dev, device_id_type=MESH)
+
+    greet({"grp": 1 - g})
+    greet({"fsdp": across})
+    greet({"fsdp": sibling})
+    pl.when(z > 0)(lambda: greet({"fsdp": left}))
+    pl.when(z < line - 1)(lambda: greet({"fsdp": right}))
+
+    lane = lax.broadcasted_iota(jnp.int32, (rows, HS), 1)
+
+    def row_sums(first, second):
+        return jnp.where(
+            lane == 0,
+            jnp.sum(first, axis=1, keepdims=True),
+            jnp.sum(second, axis=1, keepdims=True),
+        )
+
+    wv_f = wv[...].astype(F32)
+    wo_f = wo[...].astype(F32)
+    nrm[0] = row_sums(wv_f * wv_f, wo_f * wo_f)
+    pl.semaphore_wait(
+        barrier, 3 + (z > 0).astype(jnp.int32) + (z < line - 1).astype(jnp.int32)
+    )
+    norm_copy = scopy(nrm.at[0], nrm.at[1], 0)
+    norm_copy.start()
+
+    def cols(h):
+        return pl.ds(pl.multiple_of(h * HS, HS), HS)
+
+    def probs_head(h):
+        qh = q[:, cols(h)]
+        kh = k[:, cols(h)]
+        for r in range(tokens // BLOCK):
+            top, reach = r * BLOCK, (r + 1) * BLOCK
+            scores = contract_last(qh[top:reach], kh[:reach]) * score_scale
+            row_pos = lax.broadcasted_iota(jnp.int32, (BLOCK, reach), 0) + top
+            col_pos = lax.broadcasted_iota(jnp.int32, (BLOCK, reach), 1)
+            scores = jnp.where(row_pos >= col_pos, scores, -1e30)
+            terms = jnp.exp(scores - jnp.max(scores, axis=1, keepdims=True))
+            total = jnp.sum(terms, axis=1, keepdims=True)
+            probs[h, top:reach, :reach] = (terms * (1.0 / total)).astype(BF)
+
+    probs_head(0)
+    norm_copy.wait()
+    inv = lax.rsqrt(nrm[0] + nrm[1] + EPS)
+
+    def my_rows(ref):
+        return ref.at[pl.ds(pl.multiple_of(me * rows, rows), rows)]
+
+    my_rows(all_v)[...] = (wv[...].astype(F32) * inv[:, 0:1]).astype(BF)
+    my_rows(all_o)[...] = (wo[...].astype(F32) * inv[:, 1:2]).astype(BF)
+
+    def shard(ref, u, yy, cc):
+        start = pl.multiple_of((u * 4 + yy * 2 + cc) * rows, rows)
+        return ref.at[pl.ds(start, rows)]
+
+    def unit_rows(ref, u):
+        return ref.at[pl.ds(pl.multiple_of(u * unit, unit), unit)]
+
+    gathered = (all_v, all_o)
+
+    def go_line(w, u, way, dev):
+        block = shard(gathered[w], u, y, c)
+        return copy(block, block, z_out.at[w, u, way], z_in.at[w, u], {"fsdp": dev})
+
+    def go_across(w, u):
+        block = shard(gathered[w], u, y, c)
+        return copy(block, block, y_out.at[w, u], y_in.at[w, u], {"fsdp": across})
+
+    def from_across(w, u):
+        block = shard(gathered[w], u, 1 - y, c)
+        return copy(block, block, y_out.at[w, u], y_in.at[w, u], {"fsdp": across})
+
+    def go_sibling(w, u, yy):
+        block = shard(gathered[w], u, yy, c)
+        return copy(block, block, c_out.at[w, u, yy], c_in.at[w, u, yy], {"fsdp": sibling})
+
+    def from_sibling(w, u, yy):
+        block = shard(gathered[w], u, yy, 1 - c)
+        return copy(block, block, c_out.at[w, u, yy], c_in.at[w, u, yy], {"fsdp": sibling})
+
+    def on_line(w, u, act):
+        pl.when((u <= z) & (z < line - 1))(lambda: act(go_line(w, u, 1, right)))
+        pl.when((u >= z) & (z > 0))(lambda: act(go_line(w, u, 0, left)))
+
+    def gather_step(w, s):
+        u = nearest(z, s, line)
+        if s:
+            go_line(w, u, 0, left).wait_recv()
+        on_line(w, u, lambda d: d.start())
+        go_across(w, u).start()
+        go_sibling(w, u, y).start()
+
+    def gather_across(w, s):
+        u = nearest(z, s, line)
+        from_across(w, u).wait_recv()
+        go_sibling(w, u, 1 - y).start()
+
+    def gather_sibling(w, s):
+        u = nearest(z, s, line)
+        from_sibling(w, u, 0).wait_recv()
+        from_sibling(w, u, 1).wait_recv()
+
+    def gather_drain(w):
+        def one(u, carry):
+            on_line(w, u, lambda d: d.wait_send())
+            go_across(w, u).wait_send()
+            go_sibling(w, u, 0).wait_send()
+            go_sibling(w, u, 1).wait_send()
+            return carry
+
+        lax.fori_loop(0, line, one, 0)
+
+    def is_own(u):
+        return (u >= low) & (u < low + own_units)
+
+    def split_heads(kind, u, block):
+        @pl.when(is_own(u))
+        def _():
+            for j in range(per_unit):
+                part[(u - low) * per_unit + j] = block[:, j * HS : (j + 1) * HS]
+
+        @pl.when(jnp.logical_not(is_own(u)))
+        def _():
+            for j in range(per_unit):
+                h = (u - other_low) * per_unit + j
+                xsend[kind, h] = block[:, j * HS : (j + 1) * HS].astype(BF)
+                xcopy(xsend.at[kind, h], xrecv.at[kind, h], 2 * kind, h).start()
+
+    def value_unit(s):
+        u = nearest(z, s, line)
+        split_heads(0, u, contract_last(hid[...], unit_rows(all_v, u)[...]))
+
+    gather_step(0, 0)
+    todo = list(range(1, heads))
+    for s in range(1, line):
+        while todo and len(todo) > heads - 1 - 2 * s:
+            probs_head(todo.pop(0))
+        gather_step(0, s)
+        gather_across(0, s - 1)
+        gather_sibling(0, s - 1)
+        value_unit(s - 1)
+    for h in todo:
+        probs_head(h)
+    gather_step(1, 0)
+    gather_across(0, line - 1)
+    gather_sibling(0, line - 1)
+    value_unit(line - 1)
+
+    def attend_head(h):
+        xcopy(xsend.at[0, h], xrecv.at[0, h], 0, h).wait_recv()
+        vals[h] = (part[h] + xrecv[0, h].astype(F32)).astype(BF)
+        mine = g * heads + h
+        for r in range(tokens // BLOCK):
+            top, reach = r * BLOCK, (r + 1) * BLOCK
+            attn[mine, top:reach] = jnp.dot(
+                probs[h, top:reach, :reach], vals[h, :reach], preferred_element_type=F32
+            ).astype(BF)
+        xcopy(attn.at[mine], attn.at[mine], 1, h).start()
+
+    def own_near(n):
+        zc = jnp.clip(z, low, low + own_units - 1) - low
+        return nearest(zc, n, own_units)
+
+    for n in range(own_units):
+        u = own_near(n)
+        lax.fori_loop(0, per_unit, lambda j, x: (attend_head(u * per_unit + j), x)[1], 0)
+        gather_step(1, 1 + n)
+        gather_across(1, n)
+
+    def heads_of(ref, u):
+        return jnp.concatenate([ref[u * per_unit + j] for j in range(per_unit)], axis=1)
+
+    def accumulate(ref, u, weight, fresh):
+        add = jnp.dot(heads_of(ref, u), unit_rows(weight, u)[...], preferred_element_type=F32)
+        if fresh:
+            proj[...] = add
+        else:
+            proj[...] += add
+
+    def project(s):
+        u = nearest(z, s, line)
+        gather_sibling(1, s)
+
+        @pl.when(jnp.logical_not(is_own(u)))
+        def _():
+            for j in range(per_unit):
+                h = (u - other_low) * per_unit + j
+                there = attn.at[(1 - g) * heads + h]
+                xcopy(there, there, 1, h).wait_recv()
+
+        accumulate(attn, u, all_o, s == 0)
+
+    for s in range(line):
+        if s + 1 > own_units and s + 1 < line:
+            gather_step(1, s + 1)
+        if s >= own_units:
+            gather_across(1, s)
+        project(s)
+
+    rates = alpha[...]
+    keep = 1.0 - rates
+    step = 16
+
+    def chunk(i):
+        return pl.ds(pl.multiple_of(i * step, step), step)
+
+    lane16 = lax.broadcasted_iota(jnp.int32, (step, HS), 1)
+
+    def moments(i, carry):
+        r = chunk(i)
+        p = proj[r]
+        kh = keep * hid[r].astype(F32)
+        ap = rates * p
+        go = og[r].astype(F32)
+        sums = (p * p, kh * kh, kh * ap, ap * ap, go * kh, go * ap)
+        out = jnp.zeros((step, HS), F32)
+        for n, term in enumerate(sums):
+            out = jnp.where(lane16 == n, jnp.sum(term, axis=1, keepdims=True), out)
+        mom[r] = out
+        return carry
+
+    lax.fori_loop(0, tokens // step, moments, 0)
+    for i in range(tokens // HS):
+        span = slice(i * HS, (i + 1) * HS)
+        momx[0, :, span] = jnp.transpose(mom[span])[:8]
+    mom_copy = scopy(momx.at[0], momx.at[1], 1)
+    mom_copy.start()
+    gather_drain(0)
+    gather_drain(1)
+    mom_copy.wait()
+    for i in range(tokens // HS):
+        span = slice(i * HS, (i + 1) * HS)
+        total = momx[0, :, span] + momx[1, :, span]
+        padded = jnp.concatenate([total, jnp.zeros((HS - 8, HS), F32)], axis=0)
+        mom[span] = jnp.transpose(padded)
+
+    def mix(i, carry):
+        r = chunk(i)
+        m = mom[r]
+        s_pp, s_hh, s_hp, s_ap, s_gh, s_gp = [m[:, n : n + 1] for n in range(6)]
+        proj_rs = lax.rsqrt(s_pp / full + EPS)
+        mix_mean = (s_hh + 2.0 * proj_rs * s_hp + proj_rs * proj_rs * s_ap) / full
+        mix_rs = lax.rsqrt(mix_mean + EPS)
+        grad_mean = (s_gh + proj_rs * s_gp) / full
+        proj_mean = (
+            mix_rs * s_gp - mix_rs * mix_rs * mix_rs * grad_mean * (s_hp + proj_rs * s_ap)
+        ) / full
+        p = proj[r]
+        pn = p * proj_rs
+        h = hid[r].astype(F32)
+        mixed = h + rates * (pn - h)
+        normed = mixed * mix_rs
+        nh[r] = normed.astype(BF)
+        grad_mix = mix_rs * (og[r].astype(F32) - normed * (mix_rs * grad_mean))
+        proj[r] = grad_mix * keep
+        gpb[r] = (proj_rs * (grad_mix * rates - pn * (proj_rs * proj_mean))).astype(BF)
+        return carry
+
+    lax.fori_loop(0, tokens // step, mix, 0)
+
+    def own_back(n):
+        return jnp.where(g == 0, n, line - 1 - n)
+
+    def other_back(n):
+        return jnp.where(g == 0, line - 1 - n, n)
+
+    for n in range(own_units):
+        u = other_back(n)
+        split_heads(1, u, contract_last(gpb[...], unit_rows(all_o, u)[...]))
+    for n in range(own_units):
+        u = own_back(n)
+        split_heads(1, u, contract_last(gpb[...], unit_rows(all_o, u)[...]))
+
+    big = (big_o, all_o)
+
+    def weight_grad(w, ref, other, u):
+        add = contract_first(heads_of(ref, u), other[...])
+        unit_rows(big[w], u)[...] = add.astype(BF)
+
+    def to_sibling(w, u, yy):
+        return copy(
+            shard(big[w], u, yy, 1 - c), ra.at[w, u, yy],
+            a_out.at[w, u, yy], a_in.at[w, u, yy], {"fsdp": sibling},
+        )
+
+    def to_across(w, u):
+        return copy(
+            ra.at[w, u, 1 - y], rb.at[w, u], b_out.at[w, u], b_in.at[w, u], {"fsdp": across}
+        )
+
+    def to_line(w, u, way, dev):
+        return copy(
+            ra.at[w, u, y], rc.at[w, u, 1 - way],
+            r_out.at[w, u, way], r_in.at[w, u, 1 - way], {"fsdp": dev},
+        )
+
+    def scatter_sibling(w, u):
+        to_sibling(w, u, 0).start()
+        to_sibling(w, u, 1).start()
+
+    def scatter_across(w, u):
+        to_sibling(w, u, 0).wait_recv()
+        to_sibling(w, u, 1).wait_recv()
+        ra[w, u, 1 - y] = (
+            ra[w, u, 1 - y].astype(F32) + shard(big[w], u, 1 - y, c)[...].astype(F32)
+        ).astype(BF)
+        to_across(w, u).start()
+
+    def scatter_line(w, u):
+        to_across(w, u).wait_recv()
+        acc[...] = (
+            shard(big[w], u, y, c)[...].astype(F32)
+            + ra[w, u, y].astype(F32)
+            + rb[w, u].astype(F32)
+        )
+
+        @pl.when((z > 0) & (u >= z))
+        def _():
+            to_line(w, u, 1, right).wait_recv()
+            acc[...] += rc[w, u, 0].astype(F32)
+
+        @pl.when((z < line - 1) & (u <= z))
+        def _():
+            to_line(w, u, 0, left).wait_recv()
+            acc[...] += rc[w, u, 1].astype(F32)
+
+        @pl.when(u == z)
+        def _():
+            fin[w] = acc[...]
+
+        @pl.when(u != z)
+        def _():
+            ra[w, u, y] = acc[...].astype(BF)
+
+        pl.when(u > z)(lambda: to_line(w, u, 1, right).start())
+        pl.when(u < z)(lambda: to_line(w, u, 0, left).start())
+
+    def scatter_drain(w):
+        def one(u, carry):
+            to_sibling(w, u, 0).wait_send()
+            to_sibling(w, u, 1).wait_send()
+            to_across(w, u).wait_send()
+            pl.when(u > z)(lambda: to_line(w, u, 1, right).wait_send())
+            pl.when(u < z)(lambda: to_line(w, u, 0, left).wait_send())
+            return carry
+
+        lax.fori_loop(0, line, one, 0)
+
+    far_first = [line - 1 - s for s in range(line)]
+    for s in far_first:
+        u = nearest(z, s, line)
+        weight_grad(0, attn, gpb, u)
+        scatter_sibling(0, u)
+
+    def back_head(h):
+        xcopy(xsend.at[1, h], xrecv.at[1, h], 2, h).wait_recv()
+        mine = g * heads + h
+        grad_head = (part[h] + xrecv[1, h].astype(F32)).astype(BF)
+        qh = q[:, cols(h)]
+        kh = k[:, cols(h)]
+        vh = vals[h]
+        for r in range(tokens // BLOCK):
+            top, reach = r * BLOCK, (r + 1) * BLOCK
+            p = probs[h, top:reach, :reach].astype(F32)
+            grad_prob = contract_last(grad_head[top:reach], vh[:reach])
+            delta = jnp.sum(p * grad_prob, axis=1, keepdims=True)
+            grad_score = (p * (grad_prob - delta)).astype(BF)
+            grad_s[top:reach, :reach] = grad_score
+            gq[top:reach, cols(h)] = (
+                jnp.dot(grad_score, kh[:reach], preferred_element_type=F32) * score_scale
+            ).astype(BF)
+        for r in range(tokens // BLOCK):
+            top, reach = r * BLOCK, (r + 1) * BLOCK
+            gval[mine, top:reach] = contract_first(
+                probs[h, top:, top:reach], grad_head[top:]
+            ).astype(BF)
+            gk[top:reach, cols(h)] = (
+                contract_first(grad_s[top:, top:reach], qh[top:]) * score_scale
+            ).astype(BF)
+        xcopy(gval.at[mine], gval.at[mine], 3, h).start()
+
+    for n in range(own_units):
+        u = own_back(n)
+        lax.fori_loop(
+            0, per_unit, lambda j, x: (back_head((u - low) * per_unit + j), x)[1], 0
+        )
+        if n == 0:
+            for s in far_first:
+                scatter_across(0, nearest(z, s, line))
+        weight_grad(1, gval, hid, u)
+        scatter_sibling(1, u)
+        if n < line:
+            scatter_line(0, nearest(z, far_first[n], line))
+    for n in range(own_units):
+        u = own_back(n)
+        scatter_across(1, u)
+        accumulate(gval, u, all_v, False)
+        if own_units + n < line:
+            scatter_line(0, nearest(z, far_first[own_units + n], line))
+
+    for n in range(own_units):
+        u = other_back(n)
+        for j in range(per_unit):
+            h = (u - other_low) * per_unit + j
+            there = gval.at[(1 - g) * heads + h]
+            xcopy(there, there, 3, h).wait_recv()
+        weight_grad(1, gval, hid, u)
+        scatter_sibling(1, u)
+        scatter_line(1, own_back(n))
+        scatter_across(1, u)
+        accumulate(gval, u, all_v, False)
+    gh[...] = proj[...].astype(BF)
+
+    inv = lax.rsqrt(nrm[0] + nrm[1] + EPS)
+    unit_v = wv[...].astype(F32) * inv[:, 0:1]
+    unit_o = wo[...].astype(F32) * inv[:, 1:2]
+    for n in range(own_units):
+        scatter_line(1, other_back(n))
+    dots[0] = row_sums(fin[1] * unit_v, fin[0] * unit_o)
+    dot_copy = scopy(dots.at[0], dots.at[1], 2)
+    dot_copy.start()
+    scatter_drain(0)
+    scatter_drain(1)
+
+    def drain(h, carry):
+        xcopy(xsend.at[0, h], xrecv.at[0, h], 0, h).wait_send()
+        xcopy(xsend.at[1, h], xrecv.at[1, h], 2, h).wait_send()
+        mine = g * heads + h
+        xcopy(attn.at[mine], attn.at[mine], 1, h).wait_send()
+        xcopy(gval.at[mine], gval.at[mine], 3, h).wait_send()
+        return carry
+
+    lax.fori_loop(0, heads, drain, 0)
+    dot_copy.wait()
+    total = dots[0] + dots[1]
+    gwv[...] = (fin[1] - unit_v * total[:, 0:1]) * inv[:, 0:1]
+    gwo[...] = (fin[0] - unit_o * total[:, 1:2]) * inv[:, 1:2]
+
+
+def layer(hidden, queries, attn_keys, w_value, w_out, alpha, out_grad):
+    tokens, width = hidden.shape
+    rows = w_value.shape[0]
+    own = queries.shape[1]
+    heads = own // HS
+    devices = lax.axis_size("fsdp")
+    line = devices // 4
+    head_block = (heads, tokens, HS)
+    dma = pltpu.SemaphoreType.DMA
+    shape = jax.ShapeDtypeStruct
+    scratch = [
+        pltpu.VMEM((devices * rows, width), BF),
+        pltpu.VMEM((devices * rows, width), BF),
+        pltpu.VMEM((heads, tokens, tokens), BF),
+        pltpu.VMEM((2, rows, HS), F32),
+        pltpu.VMEM(head_block, F32),
+        pltpu.VMEM((2,) + head_block, BF),
+        pltpu.VMEM((2,) + head_block, BF),
+        pltpu.VMEM(head_block, BF),
+        pltpu.VMEM((2 * heads, tokens, HS), BF),
+        pltpu.VMEM((tokens, width), F32),
+        pltpu.VMEM((tokens, width), BF),
+        pltpu.VMEM((tokens, HS), F32),
+        pltpu.VMEM((2, 8, tokens), F32),
+        pltpu.VMEM((2 * heads, tokens, HS), BF),
+        pltpu.VMEM((tokens, tokens), BF),
+        pltpu.VMEM((devices * rows, width), BF),
+        pltpu.VMEM((2, line, 2, rows, width), BF),
+        pltpu.VMEM((2, line, rows, width), BF),
+        pltpu.VMEM((2, line, 2, rows, width), BF),
+        pltpu.VMEM((rows, width), F32),
+        pltpu.VMEM((2, rows, width), F32),
+        pltpu.VMEM((2, rows, HS), F32),
+        dma((2, line)), dma((2, line, 2)), dma((2, line)), dma((2, line)),
+        dma((2, line, 2)), dma((2, line, 2)),
+        dma((2, line, 2)), dma((2, line, 2)), dma((2, line)), dma((2, line)),
+        dma((2, line, 2)), dma((2, line, 2)),
+        dma((4, heads)), dma((4, heads)), dma((3,)), dma((3,)),
+    ]
+    return pl.pallas_call(
+        layer_kernel,
+        in_specs=[pl.BlockSpec(memory_space=pltpu.VMEM)] * 7,
+        out_specs=[pl.BlockSpec(memory_space=pltpu.VMEM)] * 6,
+        out_shape=[
+            shape((tokens, width), BF),
+            shape((tokens, width), BF),
+            shape((tokens, own), BF),
+            shape((tokens, own), BF),
+            shape((rows, width), F32),
+            shape((rows, width), F32),
+        ],
+        scratch_shapes=scratch,
+        compiler_params=pltpu.CompilerParams(
+            collective_id=0, has_side_effects=True, vmem_limit_bytes=67043328
+        ),
+    )(hidden, queries, attn_keys, w_value, w_out, alpha[None, :], out_grad)
+
+
+def fits(queries, w_value, alpha, devices):
+    rows, own = w_value.shape[0], queries.shape[1]
+    unit = 4 * rows
+    return (
+        devices % 8 == 0
+        and rows % 16 == 0
+        and unit % HS == 0
+        and own * 2 == devices * rows
+        and own % unit == 0
+        and queries.shape[0] % BLOCK == 0
+    )
+
+
+def sublayer(hidden, queries, attn_keys, w_value, w_out, alpha, out_grad):
+    run = layer if fits(queries, w_value, alpha, lax.axis_size("fsdp")) else shards
+    return tuple(run(hidden, queries, attn_keys, w_value, w_out, alpha, out_grad))
+
+
 def solution(mesh):
     placed = (
         P("fsdp", "grp"),
@@ -237,7 +811,7 @@
         P("fsdp", "grp"),
     )
     return jax.shard_map(
-        shards,
+        sublayer,
         mesh=mesh,
         in_specs=placed,
         out_specs=(

time: 309 us -> 223 us (0.72)
  waiting for transfers between devices: 194 us -> 0 us
  Pallas kernels: 23.5 us -> 213 us
  matrix products: 37.6 us -> 0 us
  other arithmetic: 18.7 us -> 0 us
  between operations: 13.9 us -> 0.66 us
  starting transfers between devices: 13.1 us -> 0 us
  local copies, waits for them, and re-layouts: 5.67 us -> 9.14 us
    pallas_call x3 -> x1, Pallas kernels: 23.5 us -> 213 us  [layer(): pl.pallas_call(layer_kernel, in_specs=[pl.BlockSpec(memory_space=pltpu.VM...]
    reduce_scatter x2 -> x0, waiting for transfers between devices: 83.1 us -> none  [the longest x1 67.5 us: shards(): lax.psum_scatter(contract_first(grad_values, hidden).astype(jnp.bfloat16)...]
    ppermute x9 -> x0, waiting for transfers between devices: 66.4 us -> none  [exchange(): return lax.ppermute(block, 'grp', swap)]
    all_gather x2 -> x0, waiting for transfers between devices: 43.3 us -> none  [the longest x1 41.8 us: shards(): raw_v = lax.all_gather(w_value, 'fsdp', axis=0, tiled=True)]
    dot_general x8 -> x0, matrix products: 37.6 us -> none  [the longest x4 13.2 us: contract_last(): lax.dot_general(left, right, (((1,), (1,)), ((), ())), preferred_element_...]
    ppermute x9 -> x0, starting transfers between devices: 12.8 us -> none  [exchange(): return lax.ppermute(block, 'grp', swap)]
    convert_element_type x2 -> x0, other arithmetic: 6.28 us -> none  [the longest x1 4.48 us: shards(): grad_proj_b = grad_proj.astype(jnp.bfloat16)]
    reduce_sum x5 -> x0, other arithmetic: 5.7 us -> none  [the longest x1 1.23 us: shards(): dot_o = jnp.sum(gw_o_own * unit_o, axis=1, keepdims=True)]
  transfers between devices with their start and end apart: 13 -> 0, of which waited for: 11 -> 0; matrix products, arithmetic and copies ran while one was open for 12% -> 0% of each run, Pallas kernels for 8% -> 0%
where the time goes in v1:
time: 223 us
  Pallas kernels  213 us (96%)
  local copies, waits for them, and re-layouts  9.14 us (4%)
    pallas_call x1, Pallas kernels, layer(): pl.pallas_call(layer_kernel, in_specs=[pl.BlockSpec(memory_space=pltpu.VM...  213 us
    unnamed x16, local copies, waits for them, and re-layouts  7.85 us

profile of v1, /device:TPU:8, one launch (start us, length us, event | category | flops | bytes accessed | tf_op | source)
XLA Modules:
  0.0 222.7 jit_solution(17801403862344660543)
XLA Ops:
  0.6 1.3 broadcast_in_dim.3.alpha
  1.9 212.9 %shard_map.118 = (bf16[512,1536]{1,0:T(8,128)(2,1)}, bf16[512,1536]{1,0:T(8,128)(2,1)}, bf16[512,768]{1,0:T(8,128)(2,1)}, bf16[512,768]{1,0:T(8,128)(2,1)}, f32[96,1536]{1,0:T(8,128)}, /*index=5*/f32[96,1536]{1,0:T(8,128)}) custom-call(bf16[512,1536]{1,0:T(8,128)(2,1)} %hid.1, bf16[512,768]{1,0:T(8,128)(2,1)} %q.1, bf16[512,768]{1,0:T(8,128)(2,1)} %k.1, ...), custom_call_target="tpu_custom_call" | custom-call | tf_op jit(solution)/shard_map/pallas_call | solution.py:766
  214.9 0.0 copy-start
  214.9 2.8 %copy.19 = bf16[512,1536]{1,0:T(8,128)(2,1)} copy(bf16[512,1536]{1,0:T(8,128)(2,1)} %get-tuple-element.12) | data formatting | bytes 3145728
  217.6 0.0 copy-done
  217.6 0.0 copy-start.2
  217.6 0.0 copy-start.1
  217.6 1.1 copy.20
  218.8 0.5 copy-done.2
  219.3 0.0 copy-start.4
  219.3 0.9 copy.21
  220.2 0.0 copy-done.1
  220.2 0.0 copy-start.3
  220.2 0.9 copy.22
  221.1 0.0 copy-done.4
  221.1 0.8 copy.23
  221.9 0.0 copy-done.3
  221.9 0.8 copy.24
Async XLA Ops:
  214.9 2.8 %copy-start = (bf16[512,1536]{1,0:T(8,128)(2,1)S(1)}, bf16[512,1536]{1,0:T(8,128)(2,1)}, u32[]{:S(2)}) copy-start(bf16[512,1536]{1,0:T(8,128)(2,1)} %get-tuple-element.13) | copy-start | bytes 4718596
  217.6 1.7 copy-start.2
  217.6 2.6 %copy-start.1 = (bf16[512,768]{1,0:T(8,128)(2,1)S(1)}, bf16[512,768]{1,0:T(8,128)(2,1)}, u32[]{:S(2)}) copy-start(bf16[512,768]{1,0:T(8,128)(2,1)} %get-tuple-element.15) | copy-start | bytes 2359300
  219.3 1.8 copy-start.4
  220.2 1.7 copy-start.3

commit v2 on v1

--- a/solution.py
+++ b/solution.py
@@ -240,12 +240,13 @@
 
 
 def layer_kernel(
-    hid, q, k, wv, wo, alpha, og,
-    nh, gh, gq, gk, gwv, gwo,
+    wv, wo, alpha, hid_hbm, q_hbm, k_hbm, og_hbm,
+    nh_hbm, gh_hbm, gq_hbm, gk_hbm, gwv_hbm, gwo_hbm,
+    hid, q, k, og, nh, gh, gq, gk, gwv, gwo, rates2,
     all_v, all_o, probs, nrm, part, xsend, xrecv, vals, attn, proj, gpb, mom, momx, gval,
     grad_s, big_o, ra, rb, rc, acc, fin, dots,
     z_in, z_out, y_in, y_out, c_in, c_out,
-    a_in, a_out, b_in, b_out, r_in, r_out, x_in, x_out, s_in, s_out,
+    a_in, a_out, b_in, b_out, r_in, r_out, x_in, x_out, s_in, s_out, load_sem, store_sem,
 ):
     tokens, width = hid.shape
     rows = wv.shape[0]
@@ -257,6 +258,21 @@
     own_units = line // 2
     score_scale = HS ** (-0.5)
     full = 2 * width
+    piece = 32 if rows % 32 == 0 else 16
+    pieces = rows // piece
+
+    loads = [
+        pltpu.make_async_copy(src, dst, load_sem.at[i])
+        for i, (src, dst) in enumerate(((q_hbm, q), (k_hbm, k), (hid_hbm, hid), (og_hbm, og)))
+    ]
+    stores = [
+        pltpu.make_async_copy(src, dst, store_sem.at[i])
+        for i, (src, dst) in enumerate(
+            ((nh, nh_hbm), (gq, gq_hbm), (gk, gk_hbm), (gh, gh_hbm), (gwv, gwv_hbm), (gwo, gwo_hbm))
+        )
+    ]
+    for load in loads:
+        load.start()
 
     me = lax.axis_index("fsdp")
     g = lax.axis_index("grp")
@@ -326,6 +342,11 @@
             total = jnp.sum(terms, axis=1, keepdims=True)
             probs[h, top:reach, :reach] = (terms * (1.0 / total)).astype(BF)
 
+    spread = jnp.broadcast_to(alpha[...][None, :], (16, width))
+    rates2[0] = spread
+    rates2[1] = 1.0 - spread
+    loads[0].wait()
+    loads[1].wait()
     probs_head(0)
     norm_copy.wait()
     inv = lax.rsqrt(nrm[0] + nrm[1] + EPS)
@@ -345,17 +366,27 @@
 
     gathered = (all_v, all_o)
 
-    def go_line(w, u, way, dev):
-        block = shard(gathered[w], u, y, c)
-        return copy(block, block, z_out.at[w, u, way], z_in.at[w, u], {"fsdp": dev})
-
-    def go_across(w, u):
-        block = shard(gathered[w], u, y, c)
-        return copy(block, block, y_out.at[w, u], y_in.at[w, u], {"fsdp": across})
-
-    def from_across(w, u):
-        block = shard(gathered[w], u, 1 - y, c)
-        return copy(block, block, y_out.at[w, u], y_in.at[w, u], {"fsdp": across})
+    def part_of(ref, p):
+        return ref.at[pl.ds(pl.multiple_of(p * piece, piece), piece)]
+
+    def shard_piece(ref, u, yy, cc, p):
+        start = pl.multiple_of((u * 4 + yy * 2 + cc) * rows + p * piece, piece)
+        return ref.at[pl.ds(start, piece)]
+
+    def each_piece(act):
+        lax.fori_loop(0, pieces, lambda p, x: (act(p), x)[1], 0)
+
+    def go_line(w, u, way, dev, p):
+        block = shard_piece(gathered[w], u, y, c, p)
+        return copy(block, block, z_out.at[w, u, way, p], z_in.at[w, u, p], {"fsdp": dev})
+
+    def go_across(w, u, p):
+        block = shard_piece(gathered[w], u, y, c, p)
+        return copy(block, block, y_out.at[w, u, p], y_in.at[w, u, p], {"fsdp": across})
+
+    def from_across(w, u, p):
+        block = shard_piece(gathered[w], u, 1 - y, c, p)
+        return copy(block, block, y_out.at[w, u, p], y_in.at[w, u, p], {"fsdp": across})
 
     def go_sibling(w, u, yy):
         block = shard(gathered[w], u, yy, c)
@@ -365,21 +396,27 @@
         block = shard(gathered[w], u, yy, 1 - c)
         return copy(block, block, c_out.at[w, u, yy], c_in.at[w, u, yy], {"fsdp": sibling})
 
-    def on_line(w, u, act):
-        pl.when((u <= z) & (z < line - 1))(lambda: act(go_line(w, u, 1, right)))
-        pl.when((u >= z) & (z > 0))(lambda: act(go_line(w, u, 0, left)))
-
-    def gather_step(w, s):
+    def on_line(w, u, p, act):
+        pl.when((u <= z) & (z < line - 1))(lambda: act(go_line(w, u, 1, right, p)))
+        pl.when((u >= z) & (z > 0))(lambda: act(go_line(w, u, 0, left, p)))
+
+    def gather_piece(w, s, p):
         u = nearest(z, s, line)
         if s:
-            go_line(w, u, 0, left).wait_recv()
-        on_line(w, u, lambda d: d.start())
-        go_across(w, u).start()
-        go_sibling(w, u, y).start()
+            go_line(w, u, 0, left, p).wait_recv()
+        on_line(w, u, p, lambda d: d.start())
+        go_across(w, u, p).start()
+
+    def gather_shard(w, s):
+        go_sibling(w, nearest(z, s, line), y).start()
+
+    def gather_step(w, s):
+        each_piece(lambda p: gather_piece(w, s, p))
+        gather_shard(w, s)
 
     def gather_across(w, s):
         u = nearest(z, s, line)
-        from_across(w, u).wait_recv()
+        each_piece(lambda p: from_across(w, u, p).wait_recv())
         go_sibling(w, u, 1 - y).start()
 
     def gather_sibling(w, s):
@@ -389,8 +426,9 @@
 
     def gather_drain(w):
         def one(u, carry):
-            on_line(w, u, lambda d: d.wait_send())
-            go_across(w, u).wait_send()
+            for p in range(pieces):
+                on_line(w, u, p, lambda d: d.wait_send())
+                go_across(w, u, p).wait_send()
             go_sibling(w, u, 0).wait_send()
             go_sibling(w, u, 1).wait_send()
             return carry
@@ -423,12 +461,15 @@
         while todo and len(todo) > heads - 1 - 2 * s:
             probs_head(todo.pop(0))
         gather_step(0, s)
+        if s == line - 1:
+            gather_step(1, 0)
         gather_across(0, s - 1)
         gather_sibling(0, s - 1)
+        if s == 1:
+            loads[2].wait()
         value_unit(s - 1)
     for h in todo:
         probs_head(h)
-    gather_step(1, 0)
     gather_across(0, line - 1)
     gather_sibling(0, line - 1)
     value_unit(line - 1)
@@ -448,10 +489,24 @@
         zc = jnp.clip(z, low, low + own_units - 1) - low
         return nearest(zc, n, own_units)
 
+    def alternate(head, step):
+        def both(j, carry):
+            head(j)
+            step(j)
+            return carry
+
+        if pieces == per_unit:
+            lax.fori_loop(0, per_unit, both, 0)
+        else:
+            lax.fori_loop(0, per_unit, lambda j, x: (head(j), x)[1], 0)
+            each_piece(step)
+
     for n in range(own_units):
         u = own_near(n)
-        lax.fori_loop(0, per_unit, lambda j, x: (attend_head(u * per_unit + j), x)[1], 0)
-        gather_step(1, 1 + n)
+        alternate(
+            lambda j: attend_head(u * per_unit + j), lambda p: gather_piece(1, 1 + n, p)
+        )
+        gather_shard(1, 1 + n)
         gather_across(1, n)
 
     def heads_of(ref, u):
@@ -477,16 +532,17 @@
 
         accumulate(attn, u, all_o, s == 0)
 
+    for s in range(own_units + 1, line):
+        gather_step(1, s)
+        gather_across(1, s - 1)
     for s in range(line):
-        if s + 1 > own_units and s + 1 < line:
-            gather_step(1, s + 1)
-        if s >= own_units:
-            gather_across(1, s)
+        if s == 1:
+            gather_across(1, line - 1)
         project(s)
 
-    rates = alpha[...]
-    keep = 1.0 - rates
     step = 16
+    inner = 4
+    loads[3].wait()
 
     def chunk(i):
         return pl.ds(pl.multiple_of(i * step, step), step)
@@ -494,19 +550,21 @@
     lane16 = lax.broadcasted_iota(jnp.int32, (step, HS), 1)
 
     def moments(i, carry):
-        r = chunk(i)
-        p = proj[r]
-        kh = keep * hid[r].astype(F32)
-        ap = rates * p
-        go = og[r].astype(F32)
-        sums = (p * p, kh * kh, kh * ap, ap * ap, go * kh, go * ap)
-        out = jnp.zeros((step, HS), F32)
-        for n, term in enumerate(sums):
-            out = jnp.where(lane16 == n, jnp.sum(term, axis=1, keepdims=True), out)
-        mom[r] = out
+        for n in range(inner):
+            r = chunk(i * inner + n)
+            rates, keep = rates2[0], rates2[1]
+            p = proj[r]
+            kh = keep * hid[r].astype(F32)
+            ap = rates * p
+            go = og[r].astype(F32)
+            sums = (p * p, kh * kh, kh * ap, ap * ap, go * kh, go * ap)
+            out = jnp.zeros((step, HS), F32)
+            for m, term in enumerate(sums):
+                out = jnp.where(lane16 == m, jnp.sum(term, axis=1, keepdims=True), out)
+            mom[r] = out
         return carry
 
-    lax.fori_loop(0, tokens // step, moments, 0)
+    lax.fori_loop(0, tokens // (step * inner), moments, 0)
     for i in range(tokens // HS):
         span = slice(i * HS, (i + 1) * HS)
         momx[0, :, span] = jnp.transpose(mom[span])[:8]
@@ -515,35 +573,40 @@
     gather_drain(0)
     gather_drain(1)
     mom_copy.wait()
+    total = momx[0] + momx[1]
+    s_pp, s_hh, s_hp, s_ap, s_gh, s_gp = [total[n : n + 1] for n in range(6)]
+    proj_rs = lax.rsqrt(s_pp / full + EPS)
+    mix_mean = (s_hh + 2.0 * proj_rs * s_hp + proj_rs * proj_rs * s_ap) / full
+    mix_rs = lax.rsqrt(mix_mean + EPS)
+    grad_mean = (s_gh + proj_rs * s_gp) / full
+    proj_mean = (
+        mix_rs * s_gp - mix_rs * mix_rs * mix_rs * grad_mean * (s_hp + proj_rs * s_ap)
+    ) / full
+    mixed_gain = mix_rs * mix_rs * mix_rs * grad_mean
+    proj_gain = proj_rs * proj_rs * proj_rs * proj_mean
     for i in range(tokens // HS):
         span = slice(i * HS, (i + 1) * HS)
-        total = momx[0, :, span] + momx[1, :, span]
-        padded = jnp.concatenate([total, jnp.zeros((HS - 8, HS), F32)], axis=0)
-        mom[span] = jnp.transpose(padded)
+        table = [v[:, span] for v in (proj_rs, mix_rs, mixed_gain, proj_gain)]
+        table.append(jnp.zeros((HS - len(table), HS), F32))
+        mom[span] = jnp.transpose(jnp.concatenate(table, axis=0))
 
     def mix(i, carry):
-        r = chunk(i)
-        m = mom[r]
-        s_pp, s_hh, s_hp, s_ap, s_gh, s_gp = [m[:, n : n + 1] for n in range(6)]
-        proj_rs = lax.rsqrt(s_pp / full + EPS)
-        mix_mean = (s_hh + 2.0 * proj_rs * s_hp + proj_rs * proj_rs * s_ap) / full
-        mix_rs = lax.rsqrt(mix_mean + EPS)
-        grad_mean = (s_gh + proj_rs * s_gp) / full
-        proj_mean = (
-            mix_rs * s_gp - mix_rs * mix_rs * mix_rs * grad_mean * (s_hp + proj_rs * s_ap)
-        ) / full
-        p = proj[r]
-        pn = p * proj_rs
-        h = hid[r].astype(F32)
-        mixed = h + rates * (pn - h)
-        normed = mixed * mix_rs
-        nh[r] = normed.astype(BF)
-        grad_mix = mix_rs * (og[r].astype(F32) - normed * (mix_rs * grad_mean))
-        proj[r] = grad_mix * keep
-        gpb[r] = (proj_rs * (grad_mix * rates - pn * (proj_rs * proj_mean))).astype(BF)
+        for n in range(inner):
+            r = chunk(i * inner + n)
+            m = mom[r]
+            rates, keep = rates2[0], rates2[1]
+            rs, ms, mg, pg = [m[:, j : j + 1] for j in range(4)]
+            p = proj[r]
+            h = hid[r].astype(F32)
+            mixed = h + rates * (p * rs - h)
+            nh[r] = (mixed * ms).astype(BF)
+            grad_mix = og[r].astype(F32) * ms - mixed * mg
+            proj[r] = grad_mix * keep
+            gpb[r] = (grad_mix * rates * rs - p * pg).astype(BF)
         return carry
 
-    lax.fori_loop(0, tokens // step, mix, 0)
+    lax.fori_loop(0, tokens // (step * inner), mix, 0)
+    stores[0].start()
 
     def own_back(n):
         return jnp.where(g == 0, n, line - 1 - n)
@@ -570,15 +633,16 @@
             a_out.at[w, u, yy], a_in.at[w, u, yy], {"fsdp": sibling},
         )
 
-    def to_across(w, u):
+    def to_across(w, u, p):
         return copy(
-            ra.at[w, u, 1 - y], rb.at[w, u], b_out.at[w, u], b_in.at[w, u], {"fsdp": across}
-        )
-
-    def to_line(w, u, way, dev):
+            part_of(ra.at[w, u, 1 - y], p), part_of(rb.at[w, u], p),
+            b_out.at[w, u, p], b_in.at[w, u, p], {"fsdp": across},
+        )
+
+    def to_line(w, u, way, dev, p):
         return copy(
-            ra.at[w, u, y], rc.at[w, u, 1 - way],
-            r_out.at[w, u, way], r_in.at[w, u, 1 - way], {"fsdp": dev},
+            part_of(ra.at[w, u, y], p), part_of(rc.at[w, u, 1 - way], p),
+            r_out.at[w, u, way, p], r_in.at[w, u, 1 - way, p], {"fsdp": dev},
         )
 
     def scatter_sibling(w, u):
@@ -588,56 +652,70 @@
     def scatter_across(w, u):
         to_sibling(w, u, 0).wait_recv()
         to_sibling(w, u, 1).wait_recv()
-        ra[w, u, 1 - y] = (
-            ra[w, u, 1 - y].astype(F32) + shard(big[w], u, 1 - y, c)[...].astype(F32)
-        ).astype(BF)
-        to_across(w, u).start()
-
-    def scatter_line(w, u):
-        to_across(w, u).wait_recv()
+
+        def one(p):
+            mine = part_of(ra.at[w, u, 1 - y], p)
+            mine[...] = (
+                mine[...].astype(F32)
+                + shard_piece(big[w], u, 1 - y, c, p)[...].astype(F32)
+            ).astype(BF)
+            to_across(w, u, p).start()
+
+        each_piece(one)
+
+    def scatter_piece(w, u, p):
+        to_across(w, u, p).wait_recv()
+        mine = part_of(ra.at[w, u, y], p)
         acc[...] = (
-            shard(big[w], u, y, c)[...].astype(F32)
-            + ra[w, u, y].astype(F32)
-            + rb[w, u].astype(F32)
+            shard_piece(big[w], u, y, c, p)[...].astype(F32)
+            + mine[...].astype(F32)
+            + part_of(rb.at[w, u], p)[...].astype(F32)
         )
 
         @pl.when((z > 0) & (u >= z))
         def _():
-            to_line(w, u, 1, right).wait_recv()
-            acc[...] += rc[w, u, 0].astype(F32)
+            to_line(w, u, 1, right, p).wait_recv()
+            acc[...] += part_of(rc.at[w, u, 0], p)[...].astype(F32)
 
         @pl.when((z < line - 1) & (u <= z))
         def _():
-            to_line(w, u, 0, left).wait_recv()
-            acc[...] += rc[w, u, 1].astype(F32)
+            to_line(w, u, 0, left, p).wait_recv()
+            acc[...] += part_of(rc.at[w, u, 1], p)[...].astype(F32)
 
         @pl.when(u == z)
         def _():
-            fin[w] = acc[...]
+            part_of(fin.at[w], p)[...] = acc[...]
 
         @pl.when(u != z)
         def _():
-            ra[w, u, y] = acc[...].astype(BF)
-
-        pl.when(u > z)(lambda: to_line(w, u, 1, right).start())
-        pl.when(u < z)(lambda: to_line(w, u, 0, left).start())
+            mine[...] = acc[...].astype(BF)
+
+        pl.when(u > z)(lambda: to_line(w, u, 1, right, p).start())
+        pl.when(u < z)(lambda: to_line(w, u, 0, left, p).start())
+
+    def scatter_line(w, u):
+        each_piece(lambda p: scatter_piece(w, u, p))
 
     def scatter_drain(w):
         def one(u, carry):
             to_sibling(w, u, 0).wait_send()
             to_sibling(w, u, 1).wait_send()
-            to_across(w, u).wait_send()
-            pl.when(u > z)(lambda: to_line(w, u, 1, right).wait_send())
-            pl.when(u < z)(lambda: to_line(w, u, 0, left).wait_send())
+            for p in range(pieces):
+                to_across(w, u, p).wait_send()
+                pl.when(u > z)(lambda: to_line(w, u, 1, right, p).wait_send())
+                pl.when(u < z)(lambda: to_line(w, u, 0, left, p).wait_send())
             return carry
 
         lax.fori_loop(0, line, one, 0)
 
     far_first = [line - 1 - s for s in range(line)]
-    for s in far_first:
+    for n, s in enumerate(far_first):
         u = nearest(z, s, line)
         weight_grad(0, attn, gpb, u)
         scatter_sibling(0, u)
+        if n:
+            scatter_across(0, nearest(z, far_first[n - 1], line))
+    scatter_across(0, nearest(z, 0, line))
 
     def back_head(h):
         xcopy(xsend.at[1, h], xrecv.at[1, h], 2, h).wait_recv()
@@ -668,22 +746,18 @@
 
     for n in range(own_units):
         u = own_back(n)
-        lax.fori_loop(
-            0, per_unit, lambda j, x: (back_head((u - low) * per_unit + j), x)[1], 0
-        )
-        if n == 0:
-            for s in far_first:
-                scatter_across(0, nearest(z, s, line))
+        far = nearest(z, far_first[n], line)
+        alternate(
+            lambda j: back_head((u - low) * per_unit + j), lambda p: scatter_piece(0, far, p)
+        )
         weight_grad(1, gval, hid, u)
         scatter_sibling(1, u)
-        if n < line:
-            scatter_line(0, nearest(z, far_first[n], line))
+        scatter_across(1, u)
+    stores[1].start()
+    stores[2].start()
     for n in range(own_units):
-        u = own_back(n)
-        scatter_across(1, u)
-        accumulate(gval, u, all_v, False)
-        if own_units + n < line:
-            scatter_line(0, nearest(z, far_first[own_units + n], line))
+        accumulate(gval, own_back(n), all_v, False)
+        scatter_line(0, nearest(z, far_first[own_units + n], line))
 
     for n in range(own_units):
         u = other_back(n)
@@ -693,16 +767,25 @@
             xcopy(there, there, 3, h).wait_recv()
         weight_grad(1, gval, hid, u)
         scatter_sibling(1, u)
-        scatter_line(1, own_back(n))
         scatter_across(1, u)
         accumulate(gval, u, all_v, False)
     gh[...] = proj[...].astype(BF)
+    stores[3].start()
 
     inv = lax.rsqrt(nrm[0] + nrm[1] + EPS)
     unit_v = wv[...].astype(F32) * inv[:, 0:1]
     unit_o = wo[...].astype(F32) * inv[:, 1:2]
-    for n in range(own_units):
-        scatter_line(1, other_back(n))
+    here = jnp.where((z < own_units) == (g == 0), 0, own_units) + jnp.minimum(z, line - 1 - z)
+
+    def line_step(n, carry):
+        m = n + (n >= here).astype(jnp.int32)
+        first = jnp.where(m < own_units, m, m - own_units)
+        from_low = (m < own_units) == (g == 0)
+        u = jnp.where(from_low, first, line - 1 - first)
+        scatter_line(1, jnp.where(n == line - 1, z, u))
+        return carry
+
+    lax.fori_loop(0, line, line_step, 0)
     dots[0] = row_sums(fin[1] * unit_v, fin[0] * unit_o)
     dot_copy = scopy(dots.at[0], dots.at[1], 2)
     dot_copy.start()
@@ -722,6 +805,46 @@
     total = dots[0] + dots[1]
     gwv[...] = (fin[1] - unit_v * total[:, 0:1]) * inv[:, 0:1]
     gwo[...] = (fin[0] - unit_o * total[:, 1:2]) * inv[:, 1:2]
+    stores[4].start()
+    stores[5].start()
+    for store in stores:
+        store.wait()
+
+
+def move_kernel(*refs):
+    count = (len(refs) - 1) // 3
+    ins, outs, held = refs[:count], refs[count : 2 * count], refs[2 * count : 3 * count]
+    sems = refs[3 * count]
+    reads, writes = [], []
+    for i in range(count):
+        half = held[i].shape[0] // 2
+        for j in range(2):
+            part = pl.ds(j * half, half)
+            reads.append(
+                pltpu.make_async_copy(ins[i].at[part], held[i].at[part], sems.at[0, i, j])
+            )
+            writes.append(
+                pltpu.make_async_copy(held[i].at[part], outs[i].at[part], sems.at[1, i, j])
+            )
+    for read in reads:
+        read.start()
+    for read, write in zip(reads, writes):
+        read.wait()
+        write.start()
+    for write in writes:
+        write.wait()
+
+
+def move_out(arrays):
+    anywhere = pl.BlockSpec(memory_space=pl.ANY)
+    return pl.pallas_call(
+        move_kernel,
+        in_specs=[anywhere] * len(arrays),
+        out_specs=[anywhere] * len(arrays),
+        out_shape=[jax.ShapeDtypeStruct(a.shape, a.dtype) for a in arrays],
+        scratch_shapes=[pltpu.VMEM(a.shape, a.dtype) for a in arrays]
+        + [pltpu.SemaphoreType.DMA((2, len(arrays), 2))],
+    )(*arrays)
 
 
 def layer(hidden, queries, attn_keys, w_value, w_out, alpha, out_grad):
@@ -734,7 +857,20 @@
     head_block = (heads, tokens, HS)
     dma = pltpu.SemaphoreType.DMA
     shape = jax.ShapeDtypeStruct
+    piece = 32 if rows % 32 == 0 else 16
+    pieces = rows // piece
     scratch = [
+        pltpu.VMEM((tokens, width), BF),
+        pltpu.VMEM((tokens, own), BF),
+        pltpu.VMEM((tokens, own), BF),
+        pltpu.VMEM((tokens, width), BF),
+        pltpu.VMEM((tokens, width), BF),
+        pltpu.VMEM((tokens, width), BF),
+        pltpu.VMEM((tokens, own), BF),
+        pltpu.VMEM((tokens, own), BF),
+        pltpu.VMEM((rows, width), F32),
+        pltpu.VMEM((rows, width), F32),
+        pltpu.VMEM((2, 16, width), F32),
         pltpu.VMEM((devices * rows, width), BF),
         pltpu.VMEM((devices * rows, width), BF),
         pltpu.VMEM((heads, tokens, tokens), BF),
@@ -754,19 +890,22 @@
         pltpu.VMEM((2, line, 2, rows, width), BF),
         pltpu.VMEM((2, line, rows, width), BF),
         pltpu.VMEM((2, line, 2, rows, width), BF),
-        pltpu.VMEM((rows, width), F32),
+        pltpu.VMEM((piece, width), F32),
         pltpu.VMEM((2, rows, width), F32),
         pltpu.VMEM((2, rows, HS), F32),
-        dma((2, line)), dma((2, line, 2)), dma((2, line)), dma((2, line)),
+        dma((2, line, pieces)), dma((2, line, 2, pieces)),
+        dma((2, line, pieces)), dma((2, line, pieces)),
         dma((2, line, 2)), dma((2, line, 2)),
-        dma((2, line, 2)), dma((2, line, 2)), dma((2, line)), dma((2, line)),
         dma((2, line, 2)), dma((2, line, 2)),
-        dma((4, heads)), dma((4, heads)), dma((3,)), dma((3,)),
+        dma((2, line, pieces)), dma((2, line, pieces)),
+        dma((2, line, 2, pieces)), dma((2, line, 2, pieces)),
+        dma((4, heads)), dma((4, heads)), dma((3,)), dma((3,)), dma((4,)), dma((6,)),
     ]
-    return pl.pallas_call(
+    anywhere = pl.BlockSpec(memory_space=pl.ANY)
+    outs = pl.pallas_call(
         layer_kernel,
-        in_specs=[pl.BlockSpec(memory_space=pltpu.VMEM)] * 7,
-        out_specs=[pl.BlockSpec(memory_space=pltpu.VMEM)] * 6,
+        in_specs=[pl.BlockSpec(memory_space=pltpu.VMEM)] * 3 + [anywhere] * 4,
+        out_specs=[anywhere] * 6,
         out_shape=[
             shape((tokens, width), BF),
             shape((tokens, width), BF),
@@ -779,7 +918,8 @@
         compiler_params=pltpu.CompilerParams(
             collective_id=0, has_side_effects=True, vmem_limit_bytes=67043328
         ),
-    )(hidden, queries, attn_keys, w_value, w_out, alpha[None, :], out_grad)
+    )(w_value, w_out, alpha, hidden, queries, attn_keys, out_grad)
+    return move_out(outs)
 
 
 def fits(queries, w_value, alpha, devices):

time: 223 us -> 167 us (0.75)
  Pallas kernels: 213 us -> 165 us
  local copies, waits for them, and re-layouts: 9.14 us -> 0 us
    pallas_call x1, Pallas kernels: 213 us -> 160 us  [layer(): pl.pallas_call(layer_kernel, in_specs=[pl.BlockSpec(memory_space=pltpu.VM...]
    unnamed x16 -> x0, local copies, waits for them, and re-layouts: 7.85 us -> none
    pallas_call x0 -> x1, Pallas kernels: none -> 5.11 us  [move_out(): pl.pallas_call(move_kernel, in_specs=[anywhere] * len(arrays), out_specs=...]
where the time goes in v2:
time: 167 us; the launch traced here: 166 us
  Pallas kernels  165 us (99%)
    pallas_call x1, Pallas kernels, layer(): pl.pallas_call(layer_kernel, in_specs=[pl.BlockSpec(memory_space=pltpu.VM...  160 us
    pallas_call x1, Pallas kernels, move_out(): pl.pallas_call(move_kernel, in_specs=[anywhere] * len(arrays), out_specs=...  5.11 us

profile of v2, /device:TPU:8, one launch (start us, length us, event | category | flops | bytes accessed | tf_op | source)
XLA Modules:
  0.0 166.1 jit_solution(727980533587399719)
XLA Ops:
  0.6 160.2 %shard_map.118 = (bf16[512,1536]{1,0:T(8,128)(2,1)}, bf16[512,1536]{1,0:T(8,128)(2,1)}, bf16[512,768]{1,0:T(8,128)(2,1)}, bf16[512,768]{1,0:T(8,128)(2,1)}, f32[96,1536]{1,0:T(8,128)}, /*index=5*/f32[96,1536]{1,0:T(8,128)}) custom-call(bf16[96,1536]{1,0:T(8,128)(2,1)} %wv.1, bf16[96,1536]{1,0:T(8,128)(2,1)} %wo.1, f32[1536]{0:T(1024)} %alpha.1, ...), custom_call_target="tpu_custom_call" | custom-call | tf_op jit(solution)/shard_map/pallas_call | solution.py:905
  160.9 5.1 %shard_map.119 = (bf16[512,1536]{1,0:T(8,128)(2,1)}, bf16[512,1536]{1,0:T(8,128)(2,1)}, bf16[512,768]{1,0:T(8,128)(2,1)}, bf16[512,768]{1,0:T(8,128)(2,1)}, f32[96,1536]{1,0:T(8,128)}, /*index=5*/f32[96,1536]{1,0:T(8,128)}) custom-call(bf16[512,1536]{1,0:T(8,128)(2,1)} %get-tuple-element.12.refs_0_, bf16[512,1536]{1,0:T(8,128)(2,1)} %get-tuple-element.13.refs_1_, ...), custom_call_target="tpu_custom_call" | custom-call | tf_op jit(solution)/shard_map/pallas_call | solution.py:840
